TPU v7x, 32 devices: a whole 2x2x4 slice. The times are simulated.
32 devices in a mesh: slab: 2 (over x), row: 8 (over z, y), col: 2 (over core).
Axes of the slice: x: 2, y: 2, z: 4, core: 2. Of those that a mesh axis runs over, the one named last changes fastest.
Arguments:
- image: float32 [1024, 4096], P(('slab', 'row'), 'col'), parts along dimension 0, may hold values from -6 to 6
Outputs:
- dog_fine: bfloat16 [4, 1024, 4096], P(None, ('slab', 'row'), 'col'), parts along dimension 1
- hessian_fine: bfloat16 [2, 1024, 4096], P(None, ('slab', 'row'), 'col'), parts along dimension 1
- dog_coarse: bfloat16 [4, 512, 2048], P(None, ('slab', 'row', 'col')), parts along dimension 1
- hessian_coarse: bfloat16 [2, 512, 2048], P(None, ('slab', 'row', 'col')), parts along dimension 1
There are 2 independent parts, one for each index of `slab`. A program takes and returns all parts, laid end to end along the dimension named above; each array names one. Nothing has to cross between parts.
All inputs are finite; a program needn't handle non-finite values.
Results may differ from a plain program's by a relative error of at most 0.0013.
Values may be sent and summed in bfloat16 or wider, within the bound.
A program may use at most 64 MiB of HBM per device.

v0:
```python
import functools

import jax
import jax.numpy as jnp
import numpy as np
from jax import lax
from jax.experimental import pallas as pl
from jax.experimental.pallas import tpu as pltpu
from jax.sharding import PartitionSpec as P

SIGMAS = [1.6 * 2.0 ** (k / 4.0) for k in range(5)]
LEVELS = 5
LANE = 128
HALF = LANE // 2
RIM = 16
CHUNK = 4
MESH = pl.DeviceIdType.MESH
BF = jnp.bfloat16
F32 = jnp.float32


def taps_at(sigma, offset):
    spread = np.arange(25, dtype=np.float64) - 12.0
    total = np.sum(np.exp(-spread * spread / (2.0 * sigma * sigma)))
    weight = np.exp(-(offset**2) / (2.0 * sigma * sigma)) / total
    return np.where(np.abs(offset) <= 12, weight, 0.0)


def halves(matrix):
    high = matrix.astype(BF)
    low = (matrix - high.astype(np.float64)).astype(BF)
    return high, low


def ring_rows(count):
    rows = np.full(count + 8, 10**6, dtype=np.float64)
    rows[: count + 1] = np.arange(count + 1)
    rows[-1] = -1
    return rows


def ring_inputs(count, before):
    total = np.arange(count, dtype=np.float64)
    return np.where(total >= count - before, total - count, total)


def vertical_matrix(out_rows, in_rows, sigma):
    return taps_at(sigma, in_rows[None, :] - out_rows[:, None])


def pad_rows(matrix, multiple):
    return np.pad(matrix, ((0, -matrix.shape[0] % multiple), (0, 0)))


def column_weights(matrix):
    high, low = halves(matrix)
    pair = np.concatenate([high, low], axis=1)
    return np.concatenate([pair, pair], axis=0)


def row_weights(matrix):
    high, low = halves(pad_rows(matrix, 16))
    return np.concatenate([high, high, low, low], axis=1)


def split(x):
    high = x.astype(BF)
    low = (x - high.astype(F32)).astype(BF)
    return high, low


def kernel(
    rows_total, image, a_fine_far, a_coarse_far, g_level_far, g_base_far,
    dog_fine, hess_fine, dog_coarse, hess_coarse,
    ext, cext, vert, lev, diff, base, a_fine, a_coarse, g_level, g_base,
    load_sem, fsend, frecv, csend, crecv,
):
    tile_rows, tile_cols = image.shape
    tiles = tile_cols // LANE
    strip = tile_rows // 4
    half_cols = tile_cols // 2
    r = lax.axis_index("row")
    c = lax.axis_index("col")
    other = 1 - c
    has_up = r > 0
    has_down = r < rows_total - 1

    load = pltpu.make_async_copy(image, ext.at[pl.ds(0, tile_rows), pl.ds(0, tile_cols)], load_sem.at[0])
    load.start()
    pairs = [(a_fine_far, a_fine), (g_base_far, g_base), (g_level_far, g_level), (a_coarse_far, a_coarse)]
    weights = [
        pltpu.make_async_copy(far, near, load_sem.at[1 + i]) for i, (far, near) in enumerate(pairs)
    ]

    barrier = pltpu.get_barrier_semaphore()

    def greet(row, col):
        pl.semaphore_signal(barrier, inc=1, device_id={"row": row, "col": col}, device_id_type=MESH)

    greet(r, other)

    @pl.when(has_up)
    def _():
        greet(r - 1, c)
        greet(r - 1, other)

    @pl.when(has_down)
    def _():
        greet(r + 1, c)
        greet(r + 1, other)

    ends = (r == 0).astype(jnp.int32) + (r == rows_total - 1).astype(jnp.int32)
    pl.semaphore_wait(barrier, 5 - 2 * ends)

    for weight in weights:
        weight.start()
    load.wait()

    def remote(src, dst, send, recv, row, col):
        return pltpu.make_async_remote_copy(
            src_ref=src, dst_ref=dst, send_sem=send, recv_sem=recv,
            device_id={"row": row, "col": col}, device_id_type=MESH,
        )

    edge = pl.ds(pl.multiple_of(other * (tile_cols - LANE), LANE), LANE)
    own = pl.ds(0, tile_cols)
    rim = pl.ds(tile_cols, LANE)
    first = pl.ds(0, RIM)
    last = pl.ds(tile_rows - RIM, RIM)
    below = pl.ds(tile_rows, RIM)
    above = pl.ds(tile_rows + RIM, RIM)
    inner = pl.ds(0, tile_rows)

    chunks = tiles // CHUNK
    span = CHUNK * LANE
    to_down, to_up = [], []
    for j in range(chunks):
        part = pl.ds(j * span, span)
        to_down.append(remote(ext.at[last, part], ext.at[above, part], fsend.at[2 * j], frecv.at[2 * j], r + 1, c))
        to_up.append(
            remote(ext.at[first, part], ext.at[below, part], fsend.at[2 * j + 1], frecv.at[2 * j + 1], r - 1, c)
        )
    n = 2 * chunks
    to_down_corner = remote(ext.at[last, edge], ext.at[above, rim], fsend.at[n], frecv.at[n], r + 1, other)
    to_up_corner = remote(ext.at[first, edge], ext.at[below, rim], fsend.at[n + 1], frecv.at[n + 1], r - 1, other)
    to_side = remote(ext.at[inner, edge], ext.at[inner, rim], fsend.at[n + 2], frecv.at[n + 2], r, other)

    @pl.when(has_down)
    def _():
        to_down_corner.start()
        to_down[0].start()

    @pl.when(has_up)
    def _():
        to_up_corner.start()
        for send in to_up:
            send.start()

    @pl.when(has_down)
    def _():
        for send in to_down[1:]:
            send.start()

    to_side.start()

    wide = tile_cols + LANE

    @pl.when(r == 0)
    def _():
        ext[above, :] = jnp.zeros((RIM, wide), F32)

    @pl.when(r == rows_total - 1)
    def _():
        ext[below, :] = jnp.zeros((RIM, wide), F32)

    cext[:, pl.ds(tile_cols, LANE)] = jnp.zeros((3 * strip, LANE), F32)

    @pl.when(jnp.logical_and(r == 0, c == 0))
    def _():
        cext[pl.ds(2 * strip, strip), own] = jnp.zeros((strip, tile_cols), F32)

    @pl.when(jnp.logical_and(r == rows_total - 1, c == 1))
    def _():
        cext[pl.ds(strip, strip), own] = jnp.zeros((strip, tile_cols), F32)

    for weight in weights:
        weight.wait()
    to_side.wait()

    @pl.when(has_up)
    def _():
        to_down_corner.wait_recv()

    @pl.when(has_down)
    def _():
        to_up_corner.wait_recv()

    lane = lax.broadcasted_iota(jnp.int32, (1, LANE), 1)

    def vertical_pass(source, matrix, edge_keep, begin, end):
        def tile_of(t):
            value = source[:, t * LANE : (t + 1) * LANE]
            if t == tiles:
                value = value * edge_keep
            return pltpu.roll(value, HALF, 1)

        rolled = {t: tile_of(t % (tiles + 1)) for t in range(begin - 1, end)}
        left = lane < HALF
        group = [jnp.where(left, rolled[t - 1], rolled[t]) for t in range(begin, end)]
        high, low = split(jnp.concatenate(group, axis=1))
        stacked = jnp.concatenate([high, low, high, low], axis=0)
        vert[pl.ds(0, matrix.shape[0]), begin * LANE : end * LANE] = jnp.dot(
            matrix[...], stacked, preferred_element_type=F32
        )

    def horizontal_pass(start, high_rows, begin, end):
        for k in range(LEVELS):
            rows = pl.ds(start + k * high_rows, high_rows)
            windows = []
            for b in range(begin, end):
                if b == tiles:
                    windows.append(
                        jnp.concatenate([vert[rows, b * LANE : (b + 1) * LANE], vert[rows, 0:LANE]], axis=1)
                    )
                else:
                    windows.append(vert[rows, b * LANE : (b + 2) * LANE])
            high, low = split(jnp.concatenate(windows, axis=0))
            product = jnp.dot(
                jnp.concatenate([high, low], axis=1), g_level[k], preferred_element_type=F32
            )
            lev[k, pl.ds(begin * high_rows, (end - begin) * high_rows), :] = (
                product[:, :LANE] + product[:, LANE:]
            )

    half_rows = tile_rows // 2

    def base_pass(begin, end):
        windows = [vert[0:half_rows, 2 * b * LANE : (2 * b + 3) * LANE] for b in range(begin, end)]
        high, low = split(jnp.concatenate(windows, axis=0))
        product = jnp.dot(
            jnp.concatenate([high, low], axis=1), g_base[...], preferred_element_type=F32
        )
        product = product[:, :LANE] + product[:, LANE:]
        for b in range(begin, end):
            base[:, b * LANE : (b + 1) * LANE] = product[
                (b - begin) * half_rows : (b - begin + 1) * half_rows
            ]

    keep = jnp.where((lane < HALF) == (c == 0), 1.0, 0.0).astype(F32)
    sends, ups, downs = [], [], []
    base_done = 0
    blocks_done = 0
    for j in range(chunks):

        @pl.when(has_up)
        def _():
            to_down[j].wait_recv()

        @pl.when(has_down)
        def _():
            to_up[j].wait_recv()

        ready = CHUNK * (j + 1) + (1 if j == chunks - 1 else 0)
        vertical_pass(ext, a_fine, keep, CHUNK * j, ready)
        base_end = (ready - 1) // 2
        base_pass(base_done, base_end)

        near = pl.ds(base_done * LANE, (base_end - base_done) * LANE)
        mine = pl.ds(
            pl.multiple_of(c * half_cols + base_done * LANE, LANE), (base_end - base_done) * LANE
        )
        top, bottom = base.at[pl.ds(0, strip), near], base.at[pl.ds(strip, strip), near]

        def slot_rows(index):
            return pl.ds(pl.multiple_of(index * strip, 8), strip)

        pair = [
            remote(top, cext.at[slot_rows(2 * other), mine], csend.at[4 * j], crecv.at[4 * j], r, other),
            remote(bottom, cext.at[slot_rows(c), mine], csend.at[4 * j + 1], crecv.at[4 * j + 1], r, other),
        ]
        up = remote(top, cext.at[slot_rows(1), mine], csend.at[4 * j + 2], crecv.at[4 * j + 2 + c], r - 1, 1)
        down = remote(bottom, cext.at[slot_rows(2), mine], csend.at[4 * j + 3], crecv.at[4 * j + 2 + c], r + 1, 0)
        sends += pair
        ups.append(up)
        downs.append(down)

        @pl.when(has_up)
        def _():
            up.start()

        @pl.when(has_down)
        def _():
            down.start()

        for send in pair:
            send.start()

        cext[slot_rows(2 * c), mine] = base[0:strip, near]
        cext[slot_rows(other), mine] = base[strip : 2 * strip, near]

        blocks_end = tiles + 1 if j == chunks - 1 else ready - 1
        horizontal_pass(half_rows, tile_rows + 8, blocks_done, blocks_end)
        base_done, blocks_done = base_end, blocks_end

    def responses(count, blocks, dog_gain, hess_gain, row_keep, edge_keep, dog, hess):
        high_rows = count + 8
        for b in range(blocks):
            rows = pl.ds(b * high_rows, high_rows)
            level = [lev[k, rows, :] for k in range(LEVELS)]
            for k in range(LEVELS - 1):
                d = level[k + 1] - level[k]
                if b < tiles:
                    dog[k, :, b * LANE : (b + 1) * LANE] = (dog_gain * d[:count]).astype(BF)
                if k in (1, 2):
                    d = d * row_keep
                    if b == tiles:
                        d = d * edge_keep
                    diff[k - 1, rows, :] = d
        if blocks == tiles:
            diff[:, pl.ds(tiles * high_rows, high_rows), :] = jnp.zeros((2, high_rows, LANE), F32)

        def block(b):
            before, after = (b - 1) % (tiles + 1), (b + 1) % (tiles + 1)
            for m in range(2):
                centre = diff[m, pl.ds(b * high_rows, high_rows), :]
                previous = diff[m, pl.ds(before * high_rows, high_rows), :]
                following = diff[m, pl.ds(after * high_rows, high_rows), :]
                right = pltpu.roll(jnp.where(lane == 0, following, centre), LANE - 1, 1)
                left = pltpu.roll(jnp.where(lane == LANE - 1, previous, centre), 1, 1)
                slope = right - left
                dxx = (right + left - 2.0 * centre)[:count]
                twice = 2.0 * centre
                dyy = (
                    pltpu.roll(centre, high_rows - 1, 0) + pltpu.roll(centre, 1, 0) - twice
                )[:count]
                dxy = (pltpu.roll(slope, high_rows - 1, 0) - pltpu.roll(slope, 1, 0))[:count] * 0.25
                hess[m, :, b * LANE : (b + 1) * LANE] = (hess_gain * (dxx * dyy - dxy * dxy)).astype(BF)

        for b in range(tiles):
            block(b)

    def row_mask(count, before, after):
        index = lax.broadcasted_iota(jnp.int32, (count + 8, 1), 0)
        gone = jnp.logical_or(
            jnp.logical_and(index == count, jnp.logical_not(after)),
            jnp.logical_and(index == count + 7, jnp.logical_not(before)),
        )
        return jnp.where(gone, 0.0, 1.0).astype(F32)

    edge_keep = jnp.where(lane == jnp.where(c == 0, 0, LANE - 1), 1.0, 0.0).astype(F32)
    responses(
        tile_rows, tiles + 1, 20.0, 5000.0,
        row_mask(tile_rows, has_up, has_down), edge_keep, dog_fine, hess_fine,
    )

    for send in sends:
        send.wait_recv()

    @pl.when(jnp.logical_or(c == 1, has_up))
    def _():
        @pl.when(jnp.logical_or(c == 0, has_down))
        def _():
            for j in range(chunks):
                for index in range(2):
                    pltpu.make_async_remote_copy(
                        src_ref=ups[j].src_ref, dst_ref=ups[j].dst_ref,
                        send_sem=csend.at[4 * j + 2], recv_sem=crecv.at[4 * j + 2 + index],
                        device_id={"row": r, "col": other}, device_id_type=MESH,
                    ).wait_recv()

    for begin in range(0, tiles, CHUNK):
        end = begin + CHUNK + (1 if begin + CHUNK == tiles else 0)
        vertical_pass(cext, a_coarse, jnp.ones((1, LANE), F32), begin, end)
    horizontal_pass(0, strip + 8, 0, tiles)
    responses(
        strip, tiles, 80.0, 200000.0,
        row_mask(strip, jnp.logical_or(has_up, c == 1), jnp.logical_or(has_down, c == 0)),
        None, dog_coarse, hess_coarse,
    )

    @pl.when(has_down)
    def _():
        to_down_corner.wait_send()
        for send in to_down + downs:
            send.wait_send()

    @pl.when(has_up)
    def _():
        to_up_corner.wait_send()
        for send in to_up + ups:
            send.wait_send()

    for send in sends:
        send.wait_send()


def solution(mesh):
    rows_total = mesh.shape["row"]

    def local(image):
        tile_rows, tile_cols = image.shape
        strip = tile_rows // 4
        tiles = tile_cols // LANE
        fine_in = ring_inputs(tile_rows + 2 * RIM, RIM)
        coarse_in = ring_inputs(3 * strip, strip)
        a_fine = row_weights(
            np.concatenate(
                [vertical_matrix(2.0 * np.arange(tile_rows // 2), fine_in, SIGMAS[4])]
                + [vertical_matrix(ring_rows(tile_rows), fine_in, s) for s in SIGMAS]
            )
        )
        a_coarse = row_weights(
            np.concatenate([vertical_matrix(ring_rows(strip), coarse_in, s) for s in SIGMAS])
        )
        window = np.arange(2 * LANE, dtype=np.float64)[:, None] - HALF
        g_level = np.stack(
            [column_weights(taps_at(s, window - np.arange(LANE)[None, :])) for s in SIGMAS]
        )
        wider = np.arange(3 * LANE, dtype=np.float64)[:, None] - HALF
        g_base = column_weights(taps_at(SIGMAS[4], wider - 2.0 * np.arange(LANE)[None, :]))

        vmem = pl.BlockSpec(memory_space=pltpu.VMEM)
        ring = tile_rows + 8
        wide = tile_cols + LANE
        chunks = tiles // CHUNK
        return pl.pallas_call(
            functools.partial(kernel, rows_total),
            out_shape=(
                jax.ShapeDtypeStruct((4, tile_rows, tile_cols), BF),
                jax.ShapeDtypeStruct((2, tile_rows, tile_cols), BF),
                jax.ShapeDtypeStruct((4, strip, tile_cols), BF),
                jax.ShapeDtypeStruct((2, strip, tile_cols), BF),
            ),
            in_specs=[pl.BlockSpec(memory_space=pltpu.HBM)] * 5,
            out_specs=(vmem,) * 4,
            scratch_shapes=[
                pltpu.VMEM((tile_rows + 2 * RIM, wide), F32),
                pltpu.VMEM((3 * strip, wide), F32),
                pltpu.VMEM((a_fine.shape[0], wide), F32),
                pltpu.VMEM((LEVELS, (tiles + 1) * ring, LANE), F32),
                pltpu.VMEM((2, (tiles + 1) * ring, LANE), F32),
                pltpu.VMEM((tile_rows // 2, tile_cols // 2), F32),
                pltpu.VMEM(a_fine.shape, BF),
                pltpu.VMEM(a_coarse.shape, BF),
                pltpu.VMEM(g_level.shape, BF),
                pltpu.VMEM(g_base.shape, BF),
                pltpu.SemaphoreType.DMA((5,)),
                pltpu.SemaphoreType.DMA((2 * chunks + 3,)),
                pltpu.SemaphoreType.DMA((2 * chunks + 3,)),
                pltpu.SemaphoreType.DMA((4 * chunks,)),
                pltpu.SemaphoreType.DMA((4 * chunks,)),
            ],
            compiler_params=pltpu.CompilerParams(
                collective_id=0, has_side_effects=True, vmem_limit_bytes=62500000
            ),
        )(image, a_fine, a_coarse, g_level, g_base)

    return jax.shard_map(
        local,
        mesh=mesh,
        in_specs=(P(("slab", "row"), "col"),),
        out_specs=(
            P(None, ("slab", "row"), "col"),
            P(None, ("slab", "row"), "col"),
            P(None, ("slab", "row", "col"), None),
            P(None, ("slab", "row", "col"), None),
        ),
        check_vma=False,
    )
```

profile of v0, /device:TPU:1, one launch (start us, length us, event | category | flops | bytes accessed | tf_op | source)
XLA Modules:
  0.0 24.1 jit_solution(9809407781292647028)
XLA Ops:
  0.6 18.9 %shard_map.84 = (bf16[4,64,2048]{2,1,0:T(8,128)(2,1)}, bf16[2,64,2048]{2,1,0:T(8,128)(2,1)}, bf16[4,16,2048]{2,1,0:T(8,128)(2,1)}, bf16[2,16,2048]{2,1,0:T(8,128)(2,1)}) custom-call(f32[64,2048]{1,0:T(8,128)} %image.1, bf16[400,384]{1,0:T(8,128)(2,1)} %constant.8.clone.a_fine_far, bf16[128,192]{1,0:T(8,128)(2,1)} %constant.9.clone.a_coarse_far, ...), custom_call_target="tpu_custom_call" | custom-call | tf_op jit(solution)/shard_map/pallas_call | solution.py:426
  19.5 0.0 copy-start
  19.6 0.0 copy-start.1
  19.6 0.0 copy-start.2
  19.6 2.4 %copy.13 = bf16[4,64,2048]{2,1,0:T(8,128)(2,1)} copy(bf16[4,64,2048]{2,1,0:T(8,128)(2,1)} %get-tuple-element.8) | data formatting | bytes 2097152
  22.0 0.0 copy-done
  22.0 0.8 %copy.14 = bf16[2,64,2048]{2,1,0:T(8,128)(2,1)} copy(bf16[2,64,2048]{2,1,0:T(8,128)(2,1)S(1)} %copy-done) | data formatting | bytes 1048576
  22.8 0.0 copy-done.1
  22.8 0.7 %copy.15 = bf16[4,16,2048]{2,1,0:T(8,128)(2,1)} copy(bf16[4,16,2048]{2,1,0:T(8,128)(2,1)S(1)} %copy-done.1) | data formatting | bytes 524288
  23.5 0.0 copy-done.2
  23.5 0.7 %copy.16 = bf16[2,16,2048]{2,1,0:T(8,128)(2,1)} copy(bf16[2,16,2048]{2,1,0:T(8,128)(2,1)S(1)} %copy-done.2) | data formatting | bytes 262144
Async XLA Ops:
  19.5 2.4 %copy-start = (bf16[2,64,2048]{2,1,0:T(8,128)(2,1)S(1)}, bf16[2,64,2048]{2,1,0:T(8,128)(2,1)}, u32[]{:S(2)}) copy-start(bf16[2,64,2048]{2,1,0:T(8,128)(2,1)} %get-tuple-element.9) | copy-start | bytes 1572868
  19.6 3.2 %copy-start.1 = (bf16[4,16,2048]{2,1,0:T(8,128)(2,1)S(1)}, bf16[4,16,2048]{2,1,0:T(8,128)(2,1)}, u32[]{:S(2)}) copy-start(bf16[4,16,2048]{2,1,0:T(8,128)(2,1)} %get-tuple-element.10) | copy-start | bytes 786436
  19.6 3.9 %copy-start.2 = (bf16[2,16,2048]{2,1,0:T(8,128)(2,1)S(1)}, bf16[2,16,2048]{2,1,0:T(8,128)(2,1)}, u32[]{:S(2)}) copy-start(bf16[2,16,2048]{2,1,0:T(8,128)(2,1)} %get-tuple-element.11) | copy-start | bytes 393220
where the time goes:
time: 24.3 us; the launch traced here: 24.1 us
  Pallas kernels  18.9 us (78%)
  local copies, waits for them, and re-layouts  4.54 us (19%)
  between operations  0.66 us (3%)
    pallas_call x1, Pallas kernels, local(): pl.pallas_call(functools.partial(kernel, rows_total), out_shape=(jax.Shap...  18.9 us
    unnamed x10, local copies, waits for them, and re-layouts  4.54 us

commit v1 on v0

--- a/solution.py
+++ b/solution.py
@@ -69,10 +69,100 @@
     return high, low
 
 
+def vertical_pass(source, matrix, vert, edge_keep, begin, end):
+    tiles = source.shape[1] // LANE - 1
+    lane = lax.broadcasted_iota(jnp.int32, (1, LANE), 1)
+
+    def tile_of(t):
+        value = source[:, t * LANE : (t + 1) * LANE]
+        if t == tiles:
+            value = value * edge_keep
+        return pltpu.roll(value, HALF, 1)
+
+    rolled = {t: tile_of(t % (tiles + 1)) for t in range(begin - 1, end)}
+    left = lane < HALF
+    group = [jnp.where(left, rolled[t - 1], rolled[t]) for t in range(begin, end)]
+    high, low = split(jnp.concatenate(group, axis=1))
+    stacked = jnp.concatenate([high, low, high, low], axis=0)
+    vert[pl.ds(0, matrix.shape[0]), begin * LANE : end * LANE] = jnp.dot(
+        matrix[...], stacked, preferred_element_type=F32
+    )
+
+def horizontal_pass(vert, g_level, lev, start, high_rows, begin, end):
+    tiles = vert.shape[1] // LANE - 1
+
+    for k in range(LEVELS):
+        rows = pl.ds(start + k * high_rows, high_rows)
+        windows = []
+        for b in range(begin, end):
+            if b == tiles:
+                windows.append(
+                    jnp.concatenate([vert[rows, b * LANE : (b + 1) * LANE], vert[rows, 0:LANE]], axis=1)
+                )
+            else:
+                windows.append(vert[rows, b * LANE : (b + 2) * LANE])
+        high, low = split(jnp.concatenate(windows, axis=0))
+        product = jnp.dot(
+            jnp.concatenate([high, low], axis=1), g_level[k], preferred_element_type=F32
+        )
+        lev[k, pl.ds(begin * high_rows, (end - begin) * high_rows), :] = (
+            product[:, :LANE] + product[:, LANE:]
+        )
+
+
+def responses(lev, diff, count, blocks, dog_gain, hess_gain, row_keep, edge_keep, dog, hess):
+    tiles = dog.shape[2] // LANE
+    lane = lax.broadcasted_iota(jnp.int32, (1, LANE), 1)
+
+    high_rows = count + 8
+    for b in range(blocks):
+        rows = pl.ds(b * high_rows, high_rows)
+        level = [lev[k, rows, :] for k in range(LEVELS)]
+        for k in range(LEVELS - 1):
+            d = level[k + 1] - level[k]
+            if b < tiles:
+                dog[k, :, b * LANE : (b + 1) * LANE] = (dog_gain * d[:count]).astype(BF)
+            if k in (1, 2):
+                d = d * row_keep
+                if b == tiles:
+                    d = d * edge_keep
+                diff[k - 1, rows, :] = d
+    if blocks == tiles:
+        diff[:, pl.ds(tiles * high_rows, high_rows), :] = jnp.zeros((2, high_rows, LANE), F32)
+
+    def block(b):
+        before, after = (b - 1) % (tiles + 1), (b + 1) % (tiles + 1)
+        for m in range(2):
+            centre = diff[m, pl.ds(b * high_rows, high_rows), :]
+            previous = diff[m, pl.ds(before * high_rows, high_rows), :]
+            following = diff[m, pl.ds(after * high_rows, high_rows), :]
+            right = pltpu.roll(jnp.where(lane == 0, following, centre), LANE - 1, 1)
+            left = pltpu.roll(jnp.where(lane == LANE - 1, previous, centre), 1, 1)
+            slope = right - left
+            dxx = (right + left - 2.0 * centre)[:count]
+            twice = 2.0 * centre
+            dyy = (
+                pltpu.roll(centre, high_rows - 1, 0) + pltpu.roll(centre, 1, 0) - twice
+            )[:count]
+            dxy = (pltpu.roll(slope, high_rows - 1, 0) - pltpu.roll(slope, 1, 0))[:count] * 0.25
+            hess[m, :, b * LANE : (b + 1) * LANE] = (hess_gain * (dxx * dyy - dxy * dxy)).astype(BF)
+
+    for b in range(tiles):
+        block(b)
+
+def row_mask(count, before, after):
+    index = lax.broadcasted_iota(jnp.int32, (count + 8, 1), 0)
+    gone = jnp.logical_or(
+        jnp.logical_and(index == count, jnp.logical_not(after)),
+        jnp.logical_and(index == count + 7, jnp.logical_not(before)),
+    )
+    return jnp.where(gone, 0.0, 1.0).astype(F32)
+
+
 def kernel(
     rows_total, image, a_fine_far, a_coarse_far, g_level_far, g_base_far,
-    dog_fine, hess_fine, dog_coarse, hess_coarse,
-    ext, cext, vert, lev, diff, base, a_fine, a_coarse, g_level, g_base,
+    dog_fine, hess_fine, cext, a_coarse, g_level,
+    ext, vert, lev, diff, base, a_fine, g_base,
     load_sem, fsend, frecv, csend, crecv,
 ):
     tile_rows, tile_cols = image.shape
@@ -197,41 +287,6 @@
 
     lane = lax.broadcasted_iota(jnp.int32, (1, LANE), 1)
 
-    def vertical_pass(source, matrix, edge_keep, begin, end):
-        def tile_of(t):
-            value = source[:, t * LANE : (t + 1) * LANE]
-            if t == tiles:
-                value = value * edge_keep
-            return pltpu.roll(value, HALF, 1)
-
-        rolled = {t: tile_of(t % (tiles + 1)) for t in range(begin - 1, end)}
-        left = lane < HALF
-        group = [jnp.where(left, rolled[t - 1], rolled[t]) for t in range(begin, end)]
-        high, low = split(jnp.concatenate(group, axis=1))
-        stacked = jnp.concatenate([high, low, high, low], axis=0)
-        vert[pl.ds(0, matrix.shape[0]), begin * LANE : end * LANE] = jnp.dot(
-            matrix[...], stacked, preferred_element_type=F32
-        )
-
-    def horizontal_pass(start, high_rows, begin, end):
-        for k in range(LEVELS):
-            rows = pl.ds(start + k * high_rows, high_rows)
-            windows = []
-            for b in range(begin, end):
-                if b == tiles:
-                    windows.append(
-                        jnp.concatenate([vert[rows, b * LANE : (b + 1) * LANE], vert[rows, 0:LANE]], axis=1)
-                    )
-                else:
-                    windows.append(vert[rows, b * LANE : (b + 2) * LANE])
-            high, low = split(jnp.concatenate(windows, axis=0))
-            product = jnp.dot(
-                jnp.concatenate([high, low], axis=1), g_level[k], preferred_element_type=F32
-            )
-            lev[k, pl.ds(begin * high_rows, (end - begin) * high_rows), :] = (
-                product[:, :LANE] + product[:, LANE:]
-            )
-
     half_rows = tile_rows // 2
 
     def base_pass(begin, end):
@@ -261,7 +316,7 @@
             to_up[j].wait_recv()
 
         ready = CHUNK * (j + 1) + (1 if j == chunks - 1 else 0)
-        vertical_pass(ext, a_fine, keep, CHUNK * j, ready)
+        vertical_pass(ext, a_fine, vert, keep, CHUNK * j, ready)
         base_end = (ready - 1) // 2
         base_pass(base_done, base_end)
 
@@ -299,57 +354,12 @@
         cext[slot_rows(other), mine] = base[strip : 2 * strip, near]
 
         blocks_end = tiles + 1 if j == chunks - 1 else ready - 1
-        horizontal_pass(half_rows, tile_rows + 8, blocks_done, blocks_end)
+        horizontal_pass(vert, g_level, lev, half_rows, tile_rows + 8, blocks_done, blocks_end)
         base_done, blocks_done = base_end, blocks_end
-
-    def responses(count, blocks, dog_gain, hess_gain, row_keep, edge_keep, dog, hess):
-        high_rows = count + 8
-        for b in range(blocks):
-            rows = pl.ds(b * high_rows, high_rows)
-            level = [lev[k, rows, :] for k in range(LEVELS)]
-            for k in range(LEVELS - 1):
-                d = level[k + 1] - level[k]
-                if b < tiles:
-                    dog[k, :, b * LANE : (b + 1) * LANE] = (dog_gain * d[:count]).astype(BF)
-                if k in (1, 2):
-                    d = d * row_keep
-                    if b == tiles:
-                        d = d * edge_keep
-                    diff[k - 1, rows, :] = d
-        if blocks == tiles:
-            diff[:, pl.ds(tiles * high_rows, high_rows), :] = jnp.zeros((2, high_rows, LANE), F32)
-
-        def block(b):
-            before, after = (b - 1) % (tiles + 1), (b + 1) % (tiles + 1)
-            for m in range(2):
-                centre = diff[m, pl.ds(b * high_rows, high_rows), :]
-                previous = diff[m, pl.ds(before * high_rows, high_rows), :]
-                following = diff[m, pl.ds(after * high_rows, high_rows), :]
-                right = pltpu.roll(jnp.where(lane == 0, following, centre), LANE - 1, 1)
-                left = pltpu.roll(jnp.where(lane == LANE - 1, previous, centre), 1, 1)
-                slope = right - left
-                dxx = (right + left - 2.0 * centre)[:count]
-                twice = 2.0 * centre
-                dyy = (
-                    pltpu.roll(centre, high_rows - 1, 0) + pltpu.roll(centre, 1, 0) - twice
-                )[:count]
-                dxy = (pltpu.roll(slope, high_rows - 1, 0) - pltpu.roll(slope, 1, 0))[:count] * 0.25
-                hess[m, :, b * LANE : (b + 1) * LANE] = (hess_gain * (dxx * dyy - dxy * dxy)).astype(BF)
-
-        for b in range(tiles):
-            block(b)
-
-    def row_mask(count, before, after):
-        index = lax.broadcasted_iota(jnp.int32, (count + 8, 1), 0)
-        gone = jnp.logical_or(
-            jnp.logical_and(index == count, jnp.logical_not(after)),
-            jnp.logical_and(index == count + 7, jnp.logical_not(before)),
-        )
-        return jnp.where(gone, 0.0, 1.0).astype(F32)
 
     edge_keep = jnp.where(lane == jnp.where(c == 0, 0, LANE - 1), 1.0, 0.0).astype(F32)
     responses(
-        tile_rows, tiles + 1, 20.0, 5000.0,
+        lev, diff, tile_rows, tiles + 1, 20.0, 5000.0,
         row_mask(tile_rows, has_up, has_down), edge_keep, dog_fine, hess_fine,
     )
 
@@ -368,16 +378,6 @@
                         device_id={"row": r, "col": other}, device_id_type=MESH,
                     ).wait_recv()
 
-    for begin in range(0, tiles, CHUNK):
-        end = begin + CHUNK + (1 if begin + CHUNK == tiles else 0)
-        vertical_pass(cext, a_coarse, jnp.ones((1, LANE), F32), begin, end)
-    horizontal_pass(0, strip + 8, 0, tiles)
-    responses(
-        strip, tiles, 80.0, 200000.0,
-        row_mask(strip, jnp.logical_or(has_up, c == 1), jnp.logical_or(has_down, c == 0)),
-        None, dog_coarse, hess_coarse,
-    )
-
     @pl.when(has_down)
     def _():
         to_down_corner.wait_send()
@@ -392,6 +392,40 @@
 
     for send in sends:
         send.wait_send()
+
+
+def finish(
+    rows_total, dog_near, hess_near, cext, a_coarse, g_level,
+    dog_fine, hess_fine, dog_coarse, hess_coarse,
+    vert, lev, diff, dog, hess, sem,
+):
+    strip = cext.shape[0] // 3
+    tiles = cext.shape[1] // LANE - 1
+    r = lax.axis_index("row")
+    c = lax.axis_index("col")
+    fine = [
+        pltpu.make_async_copy(dog_near, dog_fine, sem.at[0]),
+        pltpu.make_async_copy(hess_near, hess_fine, sem.at[1]),
+    ]
+    for copy in fine:
+        copy.start()
+    for begin in range(0, tiles, CHUNK):
+        end = begin + CHUNK + (1 if begin + CHUNK == tiles else 0)
+        vertical_pass(cext, a_coarse, vert, jnp.ones((1, LANE), F32), begin, end)
+    horizontal_pass(vert, g_level, lev, 0, strip + 8, 0, tiles)
+    responses(
+        lev, diff, strip, tiles, 80.0, 200000.0,
+        row_mask(strip, jnp.logical_or(r > 0, c == 1), jnp.logical_or(r < rows_total - 1, c == 0)),
+        None, dog, hess,
+    )
+    coarse = [
+        pltpu.make_async_copy(dog, dog_coarse, sem.at[2]),
+        pltpu.make_async_copy(hess, hess_coarse, sem.at[3]),
+    ]
+    for copy in coarse:
+        copy.start()
+    for copy in fine + coarse:
+        copy.wait()
 
 
 def solution(mesh):
@@ -423,26 +457,25 @@
         ring = tile_rows + 8
         wide = tile_cols + LANE
         chunks = tiles // CHUNK
-        return pl.pallas_call(
+        hbm = pl.BlockSpec(memory_space=pltpu.HBM)
+        near = pl.pallas_call(
             functools.partial(kernel, rows_total),
             out_shape=(
-                jax.ShapeDtypeStruct((4, tile_rows, tile_cols), BF),
-                jax.ShapeDtypeStruct((2, tile_rows, tile_cols), BF),
-                jax.ShapeDtypeStruct((4, strip, tile_cols), BF),
-                jax.ShapeDtypeStruct((2, strip, tile_cols), BF),
+                pltpu.VMEM((4, tile_rows, tile_cols), BF),
+                pltpu.VMEM((2, tile_rows, tile_cols), BF),
+                pltpu.VMEM((3 * strip, wide), F32),
+                pltpu.VMEM(a_coarse.shape, BF),
+                pltpu.VMEM(g_level.shape, BF),
             ),
-            in_specs=[pl.BlockSpec(memory_space=pltpu.HBM)] * 5,
-            out_specs=(vmem,) * 4,
+            in_specs=[hbm] * 5,
+            out_specs=(vmem,) * 5,
             scratch_shapes=[
                 pltpu.VMEM((tile_rows + 2 * RIM, wide), F32),
-                pltpu.VMEM((3 * strip, wide), F32),
                 pltpu.VMEM((a_fine.shape[0], wide), F32),
                 pltpu.VMEM((LEVELS, (tiles + 1) * ring, LANE), F32),
                 pltpu.VMEM((2, (tiles + 1) * ring, LANE), F32),
                 pltpu.VMEM((tile_rows // 2, tile_cols // 2), F32),
                 pltpu.VMEM(a_fine.shape, BF),
-                pltpu.VMEM(a_coarse.shape, BF),
-                pltpu.VMEM(g_level.shape, BF),
                 pltpu.VMEM(g_base.shape, BF),
                 pltpu.SemaphoreType.DMA((5,)),
                 pltpu.SemaphoreType.DMA((2 * chunks + 3,)),
@@ -451,9 +484,30 @@
                 pltpu.SemaphoreType.DMA((4 * chunks,)),
             ],
             compiler_params=pltpu.CompilerParams(
-                collective_id=0, has_side_effects=True, vmem_limit_bytes=62500000
+                collective_id=0, has_side_effects=True, vmem_limit_bytes=32000000
             ),
-        )(image, a_fine, a_coarse, g_level, g_base)
+        )(*[pltpu.with_memory_space_constraint(x, pltpu.HBM) for x in (image, a_fine, a_coarse, g_level, g_base)])
+        coarse_ring = strip + 8
+        return pl.pallas_call(
+            functools.partial(finish, rows_total),
+            out_shape=(
+                jax.ShapeDtypeStruct((4, tile_rows, tile_cols), BF),
+                jax.ShapeDtypeStruct((2, tile_rows, tile_cols), BF),
+                jax.ShapeDtypeStruct((4, strip, tile_cols), BF),
+                jax.ShapeDtypeStruct((2, strip, tile_cols), BF),
+            ),
+            in_specs=[vmem] * 5,
+            out_specs=(hbm,) * 4,
+            scratch_shapes=[
+                pltpu.VMEM((a_coarse.shape[0], wide), F32),
+                pltpu.VMEM((LEVELS, tiles * coarse_ring, LANE), F32),
+                pltpu.VMEM((2, (tiles + 1) * coarse_ring, LANE), F32),
+                pltpu.VMEM((4, strip, tile_cols), BF),
+                pltpu.VMEM((2, strip, tile_cols), BF),
+                pltpu.SemaphoreType.DMA((4,)),
+            ],
+            compiler_params=pltpu.CompilerParams(vmem_limit_bytes=32000000),
+        )(*near)
 
     return jax.shard_map(
         local,

time: 24.3 us -> 19.1 us (0.79)
  local copies, waits for them, and re-layouts: 4.54 us -> 0 us
  Pallas kernels: 18.9 us -> 18.3 us
    unnamed x10 -> x0, local copies, waits for them, and re-layouts: 4.54 us -> none
    pallas_call x1 -> x2, Pallas kernels: 18.9 us -> 18.3 us  [the longest x1 16.5 us: local(): pl.pallas_call(functools.partial(kernel, rows_total), out_shape=(pltpu.VM...]
where the time goes in v1:
time: 19.1 us; the launch traced here: 18.9 us
  Pallas kernels  18.3 us (96%)
  between operations  0.64 us (3%)
    pallas_call x1, Pallas kernels, local(): pl.pallas_call(functools.partial(kernel, rows_total), out_shape=(pltpu.VM...  16.5 us
    pallas_call x1, Pallas kernels, local(): pl.pallas_call(functools.partial(finish, rows_total), out_shape=(jax.Shap...  1.8 us

profile of v1, /device:TPU:1, one launch (start us, length us, event | category | flops | bytes accessed | tf_op | source)
XLA Modules:
  0.0 18.9 jit_solution(13281523020929392558)
XLA Ops:
  0.6 16.5 %shard_map.84 = (bf16[4,64,2048]{2,1,0:T(8,128)(2,1)S(1)}, bf16[2,64,2048]{2,1,0:T(8,128)(2,1)S(1)}, f32[48,2176]{1,0:T(8,128)S(1)}, bf16[128,192]{1,0:T(8,128)(2,1)S(1)}, bf16[5,512,256]{2,1,0:T(8,128)(2,1)S(1)}) custom-call(f32[64,2048]{1,0:T(8,128)} %image.1, bf16[400,384]{1,0:T(8,128)(2,1)} %constant.8.clone.a_fine_far, ...), custom_call_target="tpu_custom_call" | custom-call | tf_op jit(solution)/shard_map/pallas_call | solution.py:461
  17.1 1.8 %shard_map.85 = (bf16[4,64,2048]{2,1,0:T(8,128)(2,1)}, bf16[2,64,2048]{2,1,0:T(8,128)(2,1)}, bf16[4,16,2048]{2,1,0:T(8,128)(2,1)}, bf16[2,16,2048]{2,1,0:T(8,128)(2,1)}) custom-call(bf16[4,64,2048]{2,1,0:T(8,128)(2,1)S(1)} %get-tuple-element.9.dog_near, bf16[2,64,2048]{2,1,0:T(8,128)(2,1)S(1)} %get-tuple-element.10.hess_near, ...), custom_call_target="tpu_custom_call" | custom-call | tf_op jit(solution)/shard_map/pallas_call | solution.py:491

commit v2 on v1

--- a/solution.py
+++ b/solution.py
@@ -13,6 +13,8 @@
 LANE = 128
 HALF = LANE // 2
 RIM = 16
+NEED = 13
+SPARE = RIM - NEED
 CHUNK = 4
 MESH = pl.DeviceIdType.MESH
 BF = jnp.bfloat16
@@ -58,6 +60,19 @@
     return np.concatenate([pair, pair], axis=0)
 
 
+def rim_inputs(count):
+    slot = np.arange(RIM, dtype=np.float64)
+    above = np.where(slot >= SPARE, slot - RIM, slot - SPARE)
+    below = count + np.where(slot < NEED, slot, slot - NEED)
+    return np.concatenate([above, below])
+
+
+def fine_weights(own, rim):
+    high, low = halves(pad_rows(own, 16))
+    rim_high, rim_low = halves(pad_rows(rim, 16))
+    return np.concatenate([high, high, low, rim_high, rim_low], axis=1)
+
+
 def row_weights(matrix):
     high, low = halves(pad_rows(matrix, 16))
     return np.concatenate([high, high, low, low], axis=1)
@@ -67,6 +82,33 @@
     high = x.astype(BF)
     low = (x - high.astype(F32)).astype(BF)
     return high, low
+
+
+def packed(x, shift, keep_high):
+    high = x.astype(BF).astype(F32)
+    return jnp.where(keep_high, high, pltpu.roll(x - high, shift, 0)).astype(BF)
+
+
+def fine_vertical_pass(ext, rim, matrix, vert, edge_keep, begin, end):
+    tiles = ext.shape[1] // LANE - 1
+    left = lax.broadcasted_iota(jnp.int32, (1, LANE), 1) < HALF
+
+    def tile_of(t):
+        part = slice(t * LANE, (t + 1) * LANE)
+        value = jnp.concatenate([ext[:, part], rim[0, :, part].astype(F32), rim[1, :, part].astype(F32)], axis=0)
+        if t == tiles:
+            value = value * edge_keep
+        return pltpu.roll(value, HALF, 1)
+
+    rows = ext.shape[0]
+    rolled = {t: tile_of(t % (tiles + 1)) for t in range(begin - 1, end)}
+    group = jnp.concatenate([jnp.where(left, rolled[t - 1], rolled[t]) for t in range(begin, end)], axis=1)
+    high, low = split(group[:rows])
+    edges = group[rows:].astype(BF)
+    stacked = jnp.concatenate([high, low, high, edges, edges], axis=0)
+    vert[pl.ds(0, matrix.shape[0]), begin * LANE : end * LANE] = jnp.dot(
+        matrix[...], stacked, preferred_element_type=F32
+    )
 
 
 def vertical_pass(source, matrix, vert, edge_keep, begin, end):
@@ -162,7 +204,7 @@
 def kernel(
     rows_total, image, a_fine_far, a_coarse_far, g_level_far, g_base_far,
     dog_fine, hess_fine, cext, a_coarse, g_level,
-    ext, vert, lev, diff, base, a_fine, g_base,
+    ext, rim_out, rim_in, vert, lev, diff, base, a_fine, g_base,
     load_sem, fsend, frecv, csend, crecv,
 ):
     tile_rows, tile_cols = image.shape
@@ -199,12 +241,22 @@
         greet(r + 1, c)
         greet(r + 1, other)
 
-    ends = (r == 0).astype(jnp.int32) + (r == rows_total - 1).astype(jnp.int32)
-    pl.semaphore_wait(barrier, 5 - 2 * ends)
-
     for weight in weights:
         weight.start()
     load.wait()
+
+    slot = lax.broadcasted_iota(jnp.int32, (RIM, 1), 0)
+
+    def pack(j):
+        part = slice(j * CHUNK * LANE, (j + 1) * CHUNK * LANE)
+        rim_out[0, :, part] = packed(ext[0:RIM, part], NEED, slot < NEED)
+        rim_out[1, :, part] = packed(ext[tile_rows - RIM : tile_rows, part], SPARE, slot >= SPARE)
+
+    for j in range(tiles // CHUNK):
+        pack(j)
+
+    ends = (r == 0).astype(jnp.int32) + (r == rows_total - 1).astype(jnp.int32)
+    pl.semaphore_wait(barrier, 5 - 2 * ends)
 
     def remote(src, dst, send, recv, row, col):
         return pltpu.make_async_remote_copy(
@@ -215,24 +267,22 @@
     edge = pl.ds(pl.multiple_of(other * (tile_cols - LANE), LANE), LANE)
     own = pl.ds(0, tile_cols)
     rim = pl.ds(tile_cols, LANE)
-    first = pl.ds(0, RIM)
-    last = pl.ds(tile_rows - RIM, RIM)
-    below = pl.ds(tile_rows, RIM)
-    above = pl.ds(tile_rows + RIM, RIM)
     inner = pl.ds(0, tile_rows)
+    first, last, above, below = rim_out.at[0], rim_out.at[1], rim_in.at[0], rim_in.at[1]
+    whole = pl.ds(0, RIM)
 
     chunks = tiles // CHUNK
     span = CHUNK * LANE
     to_down, to_up = [], []
     for j in range(chunks):
         part = pl.ds(j * span, span)
-        to_down.append(remote(ext.at[last, part], ext.at[above, part], fsend.at[2 * j], frecv.at[2 * j], r + 1, c))
+        to_down.append(remote(last.at[whole, part], above.at[whole, part], fsend.at[2 * j], frecv.at[2 * j], r + 1, c))
         to_up.append(
-            remote(ext.at[first, part], ext.at[below, part], fsend.at[2 * j + 1], frecv.at[2 * j + 1], r - 1, c)
+            remote(first.at[whole, part], below.at[whole, part], fsend.at[2 * j + 1], frecv.at[2 * j + 1], r - 1, c)
         )
     n = 2 * chunks
-    to_down_corner = remote(ext.at[last, edge], ext.at[above, rim], fsend.at[n], frecv.at[n], r + 1, other)
-    to_up_corner = remote(ext.at[first, edge], ext.at[below, rim], fsend.at[n + 1], frecv.at[n + 1], r - 1, other)
+    to_down_corner = remote(last.at[whole, edge], above.at[whole, rim], fsend.at[n], frecv.at[n], r + 1, other)
+    to_up_corner = remote(first.at[whole, edge], below.at[whole, rim], fsend.at[n + 1], frecv.at[n + 1], r - 1, other)
     to_side = remote(ext.at[inner, edge], ext.at[inner, rim], fsend.at[n + 2], frecv.at[n + 2], r, other)
 
     @pl.when(has_down)
@@ -257,11 +307,11 @@
 
     @pl.when(r == 0)
     def _():
-        ext[above, :] = jnp.zeros((RIM, wide), F32)
+        rim_in[0, :, :] = jnp.zeros((RIM, wide), BF)
 
     @pl.when(r == rows_total - 1)
     def _():
-        ext[below, :] = jnp.zeros((RIM, wide), F32)
+        rim_in[1, :, :] = jnp.zeros((RIM, wide), BF)
 
     cext[:, pl.ds(tile_cols, LANE)] = jnp.zeros((3 * strip, LANE), F32)
 
@@ -316,7 +366,7 @@
             to_up[j].wait_recv()
 
         ready = CHUNK * (j + 1) + (1 if j == chunks - 1 else 0)
-        vertical_pass(ext, a_fine, vert, keep, CHUNK * j, ready)
+        fine_vertical_pass(ext, rim_in, a_fine, vert, keep, CHUNK * j, ready)
         base_end = (ready - 1) // 2
         base_pass(base_done, base_end)
 
@@ -435,13 +485,14 @@
         tile_rows, tile_cols = image.shape
         strip = tile_rows // 4
         tiles = tile_cols // LANE
-        fine_in = ring_inputs(tile_rows + 2 * RIM, RIM)
         coarse_in = ring_inputs(3 * strip, strip)
-        a_fine = row_weights(
-            np.concatenate(
-                [vertical_matrix(2.0 * np.arange(tile_rows // 2), fine_in, SIGMAS[4])]
-                + [vertical_matrix(ring_rows(tile_rows), fine_in, s) for s in SIGMAS]
-            )
+        fine_out = [(2.0 * np.arange(tile_rows // 2), SIGMAS[4])] + [(ring_rows(tile_rows), s) for s in SIGMAS]
+
+        def fine_matrix(inputs):
+            return np.concatenate([vertical_matrix(rows, inputs, s) for rows, s in fine_out])
+
+        a_fine = fine_weights(
+            fine_matrix(np.arange(tile_rows, dtype=np.float64)), fine_matrix(rim_inputs(tile_rows))
         )
         a_coarse = row_weights(
             np.concatenate([vertical_matrix(ring_rows(strip), coarse_in, s) for s in SIGMAS])
@@ -470,7 +521,9 @@
             in_specs=[hbm] * 5,
             out_specs=(vmem,) * 5,
             scratch_shapes=[
-                pltpu.VMEM((tile_rows + 2 * RIM, wide), F32),
+                pltpu.VMEM((tile_rows, wide), F32),
+                pltpu.VMEM((2, RIM, tile_cols), BF),
+                pltpu.VMEM((2, RIM, wide), BF),
                 pltpu.VMEM((a_fine.shape[0], wide), F32),
                 pltpu.VMEM((LEVELS, (tiles + 1) * ring, LANE), F32),
                 pltpu.VMEM((2, (tiles + 1) * ring, LANE), F32),

time: 19.1 us -> 16.2 us (0.85)
  Pallas kernels: 18.3 us -> 15.4 us
    pallas_call x1, Pallas kernels: 16.5 us -> 13.6 us  [local(): pl.pallas_call(functools.partial(kernel, rows_total), out_shape=(pltpu.VM...]
where the time goes in v2:
time: 16.2 us; the launch traced here: 16 us
  Pallas kernels  15.4 us (95%)
  between operations  0.64 us (4%)
    pallas_call x1, Pallas kernels, local(): pl.pallas_call(functools.partial(kernel, rows_total), out_shape=(pltpu.VM...  13.6 us
    pallas_call x1, Pallas kernels, local(): pl.pallas_call(functools.partial(finish, rows_total), out_shape=(jax.Shap...  1.8 us

profile of v2, /device:TPU:1, one launch (start us, length us, event | category | flops | bytes accessed | tf_op | source)
XLA Modules:
  0.0 16.0 jit_solution(2347515364299309727)
XLA Ops:
  0.6 13.6 %shard_map.84 = (bf16[4,64,2048]{2,1,0:T(8,128)(2,1)S(1)}, bf16[2,64,2048]{2,1,0:T(8,128)(2,1)S(1)}, f32[48,2176]{1,0:T(8,128)S(1)}, bf16[128,192]{1,0:T(8,128)(2,1)S(1)}, bf16[5,512,256]{2,1,0:T(8,128)(2,1)S(1)}) custom-call(f32[64,2048]{1,0:T(8,128)} %image.1, bf16[400,256]{1,0:T(8,128)(2,1)} %constant.8.clone.a_fine_far, ...), custom_call_target="tpu_custom_call" | custom-call | tf_op jit(solution)/shard_map/pallas_call | solution.py:512
  14.3 1.8 %shard_map.85 = (bf16[4,64,2048]{2,1,0:T(8,128)(2,1)}, bf16[2,64,2048]{2,1,0:T(8,128)(2,1)}, bf16[4,16,2048]{2,1,0:T(8,128)(2,1)}, bf16[2,16,2048]{2,1,0:T(8,128)(2,1)}) custom-call(bf16[4,64,2048]{2,1,0:T(8,128)(2,1)S(1)} %get-tuple-element.9.dog_near, bf16[2,64,2048]{2,1,0:T(8,128)(2,1)S(1)} %get-tuple-element.10.hess_near, ...), custom_call_target="tpu_custom_call" | custom-call | tf_op jit(solution)/shard_map/pallas_call | solution.py:544

commit v3 on v2

--- a/solution.py
+++ b/solution.py
@@ -15,6 +15,8 @@
 RIM = 16
 NEED = 13
 SPARE = RIM - NEED
+EDGE = 16
+RING = 8
 CHUNK = 4
 MESH = pl.DeviceIdType.MESH
 BF = jnp.bfloat16
@@ -41,11 +43,6 @@
     return rows
 
 
-def ring_inputs(count, before):
-    total = np.arange(count, dtype=np.float64)
-    return np.where(total >= count - before, total - count, total)
-
-
 def vertical_matrix(out_rows, in_rows, sigma):
     return taps_at(sigma, in_rows[None, :] - out_rows[:, None])
 
@@ -67,15 +64,13 @@
     return np.concatenate([above, below])
 
 
-def fine_weights(own, rim):
-    high, low = halves(pad_rows(own, 16))
-    rim_high, rim_low = halves(pad_rows(rim, 16))
-    return np.concatenate([high, high, low, rim_high, rim_low], axis=1)
-
-
-def row_weights(matrix):
-    high, low = halves(pad_rows(matrix, 16))
-    return np.concatenate([high, high, low, low], axis=1)
+def own_weights(matrix):
+    high, low = halves(matrix)
+    return np.concatenate([high, high, low], axis=1)
+
+
+def rim_weights(matrix):
+    return np.concatenate(halves(matrix), axis=1)
 
 
 def split(x):
@@ -89,67 +84,56 @@
     return jnp.where(keep_high, high, pltpu.roll(x - high, shift, 0)).astype(BF)
 
 
-def fine_vertical_pass(ext, rim, matrix, vert, edge_keep, begin, end):
-    tiles = ext.shape[1] // LANE - 1
+def half_shifted(tile_of, tiles, begin, end):
     left = lax.broadcasted_iota(jnp.int32, (1, LANE), 1) < HALF
-
-    def tile_of(t):
-        part = slice(t * LANE, (t + 1) * LANE)
-        value = jnp.concatenate([ext[:, part], rim[0, :, part].astype(F32), rim[1, :, part].astype(F32)], axis=0)
-        if t == tiles:
-            value = value * edge_keep
-        return pltpu.roll(value, HALF, 1)
-
-    rows = ext.shape[0]
-    rolled = {t: tile_of(t % (tiles + 1)) for t in range(begin - 1, end)}
-    group = jnp.concatenate([jnp.where(left, rolled[t - 1], rolled[t]) for t in range(begin, end)], axis=1)
-    high, low = split(group[:rows])
-    edges = group[rows:].astype(BF)
-    stacked = jnp.concatenate([high, low, high, edges, edges], axis=0)
-    vert[pl.ds(0, matrix.shape[0]), begin * LANE : end * LANE] = jnp.dot(
-        matrix[...], stacked, preferred_element_type=F32
-    )
-
-
-def vertical_pass(source, matrix, vert, edge_keep, begin, end):
+    rolled = {t: pltpu.roll(tile_of(t % (tiles + 1)), HALF, 1) for t in range(begin - 1, end)}
+    return jnp.concatenate([jnp.where(left, rolled[t - 1], rolled[t]) for t in range(begin, end)], axis=1)
+
+
+def own_operand(source, edge_keep, begin, end):
     tiles = source.shape[1] // LANE - 1
-    lane = lax.broadcasted_iota(jnp.int32, (1, LANE), 1)
 
     def tile_of(t):
         value = source[:, t * LANE : (t + 1) * LANE]
-        if t == tiles:
-            value = value * edge_keep
-        return pltpu.roll(value, HALF, 1)
-
-    rolled = {t: tile_of(t % (tiles + 1)) for t in range(begin - 1, end)}
-    left = lane < HALF
-    group = [jnp.where(left, rolled[t - 1], rolled[t]) for t in range(begin, end)]
-    high, low = split(jnp.concatenate(group, axis=1))
-    stacked = jnp.concatenate([high, low, high, low], axis=0)
-    vert[pl.ds(0, matrix.shape[0]), begin * LANE : end * LANE] = jnp.dot(
-        matrix[...], stacked, preferred_element_type=F32
-    )
-
-def horizontal_pass(vert, g_level, lev, start, high_rows, begin, end):
+        return value * edge_keep if t == tiles and edge_keep is not None else value
+
+    high, low = split(half_shifted(tile_of, tiles, begin, end))
+    return jnp.concatenate([high, low, high], axis=0)
+
+
+def rim_operand(rims, edge_keep, begin, end):
+    tiles = rims[0].shape[1] // LANE - 1
+
+    def tile_of(t):
+        value = jnp.concatenate([rim[:, t * LANE : (t + 1) * LANE].astype(F32) for rim in rims], axis=0)
+        return value * edge_keep if t == tiles and edge_keep is not None else value
+
+    edges = half_shifted(tile_of, tiles, begin, end).astype(BF)
+    return jnp.concatenate([edges, edges], axis=0)
+
+
+def window(vert, rows, b, tiles):
+    if b == tiles:
+        return jnp.concatenate([vert[rows, b * LANE : (b + 1) * LANE], vert[rows, 0:LANE]], axis=1)
+    return vert[rows, b * LANE : (b + 2) * LANE]
+
+
+def across(windows, weights):
+    high, low = split(jnp.concatenate(windows, axis=0))
+    product = jnp.dot(jnp.concatenate([high, low], axis=1), weights, preferred_element_type=F32)
+    return product[:, :LANE] + product[:, LANE:]
+
+
+def horizontal_pass(vert, g_level, lev, start, count, pieces, high_rows, begin, end):
     tiles = vert.shape[1] // LANE - 1
-
     for k in range(LEVELS):
-        rows = pl.ds(start + k * high_rows, high_rows)
-        windows = []
+        rows = pl.ds(start + k * count, count)
+        product = across([window(vert, rows, b, tiles) for b in range(begin, end)], g_level[k])
         for b in range(begin, end):
-            if b == tiles:
-                windows.append(
-                    jnp.concatenate([vert[rows, b * LANE : (b + 1) * LANE], vert[rows, 0:LANE]], axis=1)
-                )
-            else:
-                windows.append(vert[rows, b * LANE : (b + 2) * LANE])
-        high, low = split(jnp.concatenate(windows, axis=0))
-        product = jnp.dot(
-            jnp.concatenate([high, low], axis=1), g_level[k], preferred_element_type=F32
-        )
-        lev[k, pl.ds(begin * high_rows, (end - begin) * high_rows), :] = (
-            product[:, :LANE] + product[:, LANE:]
-        )
+            at = (b - begin) * count
+            for first, size in pieces:
+                lev[k, pl.ds(b * high_rows + first, size), :] = product[at : at + size]
+                at += size
 
 
 def responses(lev, diff, count, blocks, dog_gain, hess_gain, row_keep, edge_keep, dog, hess):
@@ -202,9 +186,9 @@
 
 
 def kernel(
-    rows_total, image, a_fine_far, a_coarse_far, g_level_far, g_base_far,
-    dog_fine, hess_fine, cext, a_coarse, g_level,
-    ext, rim_out, rim_in, vert, lev, diff, base, a_fine, g_base,
+    rows_total, image, a_fine_far, a_rim_far, a_coarse_far, g_level_far, g_base_far,
+    dog_fine, hess_fine, cext, crim, a_coarse, g_level,
+    ext, rim_out, rim_in, crim_out, vert, lev, diff, base, a_fine, a_rim, g_base,
     load_sem, fsend, frecv, csend, crecv,
 ):
     tile_rows, tile_cols = image.shape
@@ -219,7 +203,9 @@
 
     load = pltpu.make_async_copy(image, ext.at[pl.ds(0, tile_rows), pl.ds(0, tile_cols)], load_sem.at[0])
     load.start()
-    pairs = [(a_fine_far, a_fine), (g_base_far, g_base), (g_level_far, g_level), (a_coarse_far, a_coarse)]
+    pairs = [
+        (a_fine_far, a_fine), (g_level_far, g_level), (g_base_far, g_base), (a_rim_far, a_rim), (a_coarse_far, a_coarse)
+    ]
     weights = [
         pltpu.make_async_copy(far, near, load_sem.at[1 + i]) for i, (far, near) in enumerate(pairs)
     ]
@@ -241,9 +227,9 @@
         greet(r + 1, c)
         greet(r + 1, other)
 
+    load.wait()
     for weight in weights:
         weight.start()
-    load.wait()
 
     slot = lax.broadcasted_iota(jnp.int32, (RIM, 1), 0)
 
@@ -313,20 +299,60 @@
     def _():
         rim_in[1, :, :] = jnp.zeros((RIM, wide), BF)
 
-    cext[:, pl.ds(tile_cols, LANE)] = jnp.zeros((3 * strip, LANE), F32)
-
-    @pl.when(jnp.logical_and(r == 0, c == 0))
-    def _():
-        cext[pl.ds(2 * strip, strip), own] = jnp.zeros((strip, tile_cols), F32)
-
-    @pl.when(jnp.logical_and(r == rows_total - 1, c == 1))
-    def _():
-        cext[pl.ds(strip, strip), own] = jnp.zeros((strip, tile_cols), F32)
+    cext[:, pl.ds(tile_cols, LANE)] = jnp.zeros((2 * strip, LANE), F32)
+    crim[:, pl.ds(tile_cols, LANE)] = jnp.zeros((RIM, LANE), BF)
+
+    @pl.when(jnp.logical_or(jnp.logical_and(r == 0, c == 0), jnp.logical_and(r == rows_total - 1, c == 1)))
+    def _():
+        crim[:, own] = jnp.zeros((RIM, tile_cols), BF)
 
     for weight in weights:
         weight.wait()
     to_side.wait()
 
+    lane = lax.broadcasted_iota(jnp.int32, (1, LANE), 1)
+    keep = jnp.where((lane < HALF) == (c == 0), 1.0, 0.0).astype(F32)
+    half_rows = tile_rows // 2
+    base_edge = EDGE // 2
+    high_rows = tile_rows + RING
+    edge_rows = 2 * EDGE + RING
+    edge_pieces = [(0, EDGE), (tile_rows - EDGE, EDGE + RING)]
+    middle_rows = tile_rows - 2 * EDGE
+    middle_at = a_rim.shape[0]
+
+    def base_pass(start, count, pieces, begin, end):
+        rows = pl.ds(start, count)
+        product = across([vert[rows, 2 * b * LANE : (2 * b + 3) * LANE] for b in range(begin, end)], g_base[...])
+        for b in range(begin, end):
+            at = (b - begin) * count
+            for first_row, size in pieces:
+                base[pl.ds(first_row, size), b * LANE : (b + 1) * LANE] = product[at : at + size]
+                at += size
+
+    def own_pass(begin, end):
+        vert[:, begin * LANE : end * LANE] = jnp.dot(
+            a_fine[...], own_operand(ext, keep, begin, end), preferred_element_type=F32
+        )
+
+    def rim_pass(begin, end):
+        vert[0:middle_at, begin * LANE : end * LANE] += jnp.dot(
+            a_rim[...], rim_operand(rim_in_pair, keep, begin, end), preferred_element_type=F32
+        )
+
+    rim_in_pair = [above, below]
+    ready_at = [CHUNK * (j + 1) + (1 if j == chunks - 1 else 0) for j in range(chunks)]
+    base_at = [0] + [(ready - 1) // 2 for ready in ready_at]
+    block_at = [0] + [ready - 1 for ready in ready_at[:-1]] + [tiles + 1]
+    for j in range(chunks):
+        own_pass(CHUNK * j, ready_at[j])
+        base_pass(
+            middle_at, half_rows - 2 * base_edge, [(base_edge, half_rows - 2 * base_edge)], base_at[j], base_at[j + 1]
+        )
+        horizontal_pass(
+            vert, g_level, lev, middle_at + half_rows - 2 * base_edge, middle_rows,
+            [(EDGE, middle_rows)], high_rows, block_at[j], block_at[j + 1],
+        )
+
     @pl.when(has_up)
     def _():
         to_down_corner.wait_recv()
@@ -335,26 +361,7 @@
     def _():
         to_up_corner.wait_recv()
 
-    lane = lax.broadcasted_iota(jnp.int32, (1, LANE), 1)
-
-    half_rows = tile_rows // 2
-
-    def base_pass(begin, end):
-        windows = [vert[0:half_rows, 2 * b * LANE : (2 * b + 3) * LANE] for b in range(begin, end)]
-        high, low = split(jnp.concatenate(windows, axis=0))
-        product = jnp.dot(
-            jnp.concatenate([high, low], axis=1), g_base[...], preferred_element_type=F32
-        )
-        product = product[:, :LANE] + product[:, LANE:]
-        for b in range(begin, end):
-            base[:, b * LANE : (b + 1) * LANE] = product[
-                (b - begin) * half_rows : (b - begin + 1) * half_rows
-            ]
-
-    keep = jnp.where((lane < HALF) == (c == 0), 1.0, 0.0).astype(F32)
     sends, ups, downs = [], [], []
-    base_done = 0
-    blocks_done = 0
     for j in range(chunks):
 
         @pl.when(has_up)
@@ -365,29 +372,26 @@
         def _():
             to_up[j].wait_recv()
 
-        ready = CHUNK * (j + 1) + (1 if j == chunks - 1 else 0)
-        fine_vertical_pass(ext, rim_in, a_fine, vert, keep, CHUNK * j, ready)
-        base_end = (ready - 1) // 2
-        base_pass(base_done, base_end)
-
-        near = pl.ds(base_done * LANE, (base_end - base_done) * LANE)
-        mine = pl.ds(
-            pl.multiple_of(c * half_cols + base_done * LANE, LANE), (base_end - base_done) * LANE
-        )
-        top, bottom = base.at[pl.ds(0, strip), near], base.at[pl.ds(strip, strip), near]
-
-        def slot_rows(index):
-            return pl.ds(pl.multiple_of(index * strip, 8), strip)
-
-        pair = [
-            remote(top, cext.at[slot_rows(2 * other), mine], csend.at[4 * j], crecv.at[4 * j], r, other),
-            remote(bottom, cext.at[slot_rows(c), mine], csend.at[4 * j + 1], crecv.at[4 * j + 1], r, other),
-        ]
-        up = remote(top, cext.at[slot_rows(1), mine], csend.at[4 * j + 2], crecv.at[4 * j + 2 + c], r - 1, 1)
-        down = remote(bottom, cext.at[slot_rows(2), mine], csend.at[4 * j + 3], crecv.at[4 * j + 2 + c], r + 1, 0)
-        sends += pair
+        rim_pass(CHUNK * j, ready_at[j])
+        base_pass(
+            0, 2 * base_edge, [(0, base_edge), (half_rows - base_edge, base_edge)], base_at[j], base_at[j + 1]
+        )
+
+        columns = (base_at[j + 1] - base_at[j]) * LANE
+        near = pl.ds(base_at[j] * LANE, columns)
+        mine = pl.ds(pl.multiple_of(c * half_cols + base_at[j] * LANE, LANE), columns)
+        crim_out[0, :, near] = packed(base[0:RIM, near], NEED, slot < NEED)
+        crim_out[1, :, near] = packed(base[half_rows - RIM : half_rows, near], SPARE, slot >= SPARE)
+        up = remote(
+            crim_out.at[0, :, near], crim.at[:, mine], csend.at[3 * j], crecv.at[3 * j + c], r - 1, 1
+        )
+        down = remote(
+            crim_out.at[1, :, near], crim.at[:, mine], csend.at[3 * j + 1], crecv.at[3 * j + c], r + 1, 0
+        )
+        pair = remote(base.at[:, near], cext.at[:, mine], csend.at[3 * j + 2], crecv.at[3 * j + 2], r, other)
         ups.append(up)
         downs.append(down)
+        sends.append(pair)
 
         @pl.when(has_up)
         def _():
@@ -397,15 +401,11 @@
         def _():
             down.start()
 
-        for send in pair:
-            send.start()
-
-        cext[slot_rows(2 * c), mine] = base[0:strip, near]
-        cext[slot_rows(other), mine] = base[strip : 2 * strip, near]
-
-        blocks_end = tiles + 1 if j == chunks - 1 else ready - 1
-        horizontal_pass(vert, g_level, lev, half_rows, tile_rows + 8, blocks_done, blocks_end)
-        base_done, blocks_done = base_end, blocks_end
+        pair.start()
+        cext[:, mine] = base[:, near]
+        horizontal_pass(
+            vert, g_level, lev, 2 * base_edge, edge_rows, edge_pieces, high_rows, block_at[j], block_at[j + 1]
+        )
 
     edge_keep = jnp.where(lane == jnp.where(c == 0, 0, LANE - 1), 1.0, 0.0).astype(F32)
     responses(
@@ -424,7 +424,7 @@
                 for index in range(2):
                     pltpu.make_async_remote_copy(
                         src_ref=ups[j].src_ref, dst_ref=ups[j].dst_ref,
-                        send_sem=csend.at[4 * j + 2], recv_sem=crecv.at[4 * j + 2 + index],
+                        send_sem=csend.at[3 * j], recv_sem=crecv.at[3 * j + index],
                         device_id={"row": r, "col": other}, device_id_type=MESH,
                     ).wait_recv()
 
@@ -445,11 +445,11 @@
 
 
 def finish(
-    rows_total, dog_near, hess_near, cext, a_coarse, g_level,
+    rows_total, dog_near, hess_near, cext, crim, a_coarse, g_level,
     dog_fine, hess_fine, dog_coarse, hess_coarse,
     vert, lev, diff, dog, hess, sem,
 ):
-    strip = cext.shape[0] // 3
+    strip = cext.shape[0] // 2
     tiles = cext.shape[1] // LANE - 1
     r = lax.axis_index("row")
     c = lax.axis_index("col")
@@ -461,8 +461,11 @@
         copy.start()
     for begin in range(0, tiles, CHUNK):
         end = begin + CHUNK + (1 if begin + CHUNK == tiles else 0)
-        vertical_pass(cext, a_coarse, vert, jnp.ones((1, LANE), F32), begin, end)
-    horizontal_pass(vert, g_level, lev, 0, strip + 8, 0, tiles)
+        operand = jnp.concatenate(
+            [own_operand(cext, None, begin, end), rim_operand([crim], None, begin, end)], axis=0
+        )
+        vert[:, begin * LANE : end * LANE] = jnp.dot(a_coarse[c], operand, preferred_element_type=F32)
+    horizontal_pass(vert, g_level, lev, 0, strip + RING, [(0, strip + RING)], strip + RING, 0, tiles)
     responses(
         lev, diff, strip, tiles, 80.0, 200000.0,
         row_mask(strip, jnp.logical_or(r > 0, c == 1), jnp.logical_or(r < rows_total - 1, c == 0)),
@@ -485,21 +488,47 @@
         tile_rows, tile_cols = image.shape
         strip = tile_rows // 4
         tiles = tile_cols // LANE
-        coarse_in = ring_inputs(3 * strip, strip)
-        fine_out = [(2.0 * np.arange(tile_rows // 2), SIGMAS[4])] + [(ring_rows(tile_rows), s) for s in SIGMAS]
-
-        def fine_matrix(inputs):
-            return np.concatenate([vertical_matrix(rows, inputs, s) for rows, s in fine_out])
-
-        a_fine = fine_weights(
-            fine_matrix(np.arange(tile_rows, dtype=np.float64)), fine_matrix(rim_inputs(tile_rows))
-        )
-        a_coarse = row_weights(
-            np.concatenate([vertical_matrix(ring_rows(strip), coarse_in, s) for s in SIGMAS])
-        )
-        window = np.arange(2 * LANE, dtype=np.float64)[:, None] - HALF
+        base_edge = EDGE // 2
+        half_rows = tile_rows // 2
+        numbers = np.arange(half_rows, dtype=np.float64)
+        level_rows = ring_rows(tile_rows)
+
+        def fine_matrix(base_rows, rows, inputs):
+            matrix = np.concatenate(
+                [vertical_matrix(2.0 * base_rows, inputs, SIGMAS[4])]
+                + [vertical_matrix(rows, inputs, s) for s in SIGMAS]
+            )
+            return pad_rows(matrix, 16)
+
+        def edges_of(x, edge, length):
+            return np.concatenate([x[:edge], x[length - edge :]])
+
+        fine_in = np.arange(tile_rows, dtype=np.float64)
+        edge_out = edges_of(numbers, base_edge, half_rows), edges_of(level_rows, EDGE, tile_rows)
+        middle_out = numbers[base_edge : half_rows - base_edge], level_rows[EDGE : tile_rows - EDGE]
+        a_fine = own_weights(np.concatenate([fine_matrix(*edge_out, fine_in), fine_matrix(*middle_out, fine_in)]))
+        a_rim = rim_weights(fine_matrix(*edge_out, rim_inputs(tile_rows)))
+        coarse_out = [strip * c + ring_rows(strip) for c in range(2)]
+        coarse_rim = [rim_inputs(2 * strip)[:RIM], rim_inputs(2 * strip)[RIM:]]
+
+        def coarse_matrix(c, inputs):
+            return pad_rows(np.concatenate([vertical_matrix(coarse_out[c], inputs, s) for s in SIGMAS]), 16)
+
+        a_coarse = np.stack(
+            [
+                np.concatenate(
+                    [
+                        own_weights(coarse_matrix(c, np.arange(2 * strip, dtype=np.float64))),
+                        rim_weights(coarse_matrix(c, coarse_rim[c])),
+                    ],
+                    axis=1,
+                )
+                for c in range(2)
+            ]
+        )
+        span = np.arange(2 * LANE, dtype=np.float64)[:, None] - HALF
         g_level = np.stack(
-            [column_weights(taps_at(s, window - np.arange(LANE)[None, :])) for s in SIGMAS]
+            [column_weights(taps_at(s, span - np.arange(LANE)[None, :])) for s in SIGMAS]
         )
         wider = np.arange(3 * LANE, dtype=np.float64)[:, None] - HALF
         g_base = column_weights(taps_at(SIGMAS[4], wider - 2.0 * np.arange(LANE)[None, :]))
@@ -514,32 +543,35 @@
             out_shape=(
                 pltpu.VMEM((4, tile_rows, tile_cols), BF),
                 pltpu.VMEM((2, tile_rows, tile_cols), BF),
-                pltpu.VMEM((3 * strip, wide), F32),
+                pltpu.VMEM((2 * strip, wide), F32),
+                pltpu.VMEM((RIM, wide), BF),
                 pltpu.VMEM(a_coarse.shape, BF),
                 pltpu.VMEM(g_level.shape, BF),
             ),
-            in_specs=[hbm] * 5,
-            out_specs=(vmem,) * 5,
+            in_specs=[hbm] * 6,
+            out_specs=(vmem,) * 6,
             scratch_shapes=[
                 pltpu.VMEM((tile_rows, wide), F32),
                 pltpu.VMEM((2, RIM, tile_cols), BF),
                 pltpu.VMEM((2, RIM, wide), BF),
+                pltpu.VMEM((2, RIM, tile_cols // 2), BF),
                 pltpu.VMEM((a_fine.shape[0], wide), F32),
                 pltpu.VMEM((LEVELS, (tiles + 1) * ring, LANE), F32),
                 pltpu.VMEM((2, (tiles + 1) * ring, LANE), F32),
                 pltpu.VMEM((tile_rows // 2, tile_cols // 2), F32),
                 pltpu.VMEM(a_fine.shape, BF),
+                pltpu.VMEM(a_rim.shape, BF),
                 pltpu.VMEM(g_base.shape, BF),
-                pltpu.SemaphoreType.DMA((5,)),
+                pltpu.SemaphoreType.DMA((6,)),
                 pltpu.SemaphoreType.DMA((2 * chunks + 3,)),
                 pltpu.SemaphoreType.DMA((2 * chunks + 3,)),
-                pltpu.SemaphoreType.DMA((4 * chunks,)),
-                pltpu.SemaphoreType.DMA((4 * chunks,)),
+                pltpu.SemaphoreType.DMA((3 * chunks,)),
+                pltpu.SemaphoreType.DMA((3 * chunks,)),
             ],
             compiler_params=pltpu.CompilerParams(
                 collective_id=0, has_side_effects=True, vmem_limit_bytes=32000000
             ),
-        )(*[pltpu.with_memory_space_constraint(x, pltpu.HBM) for x in (image, a_fine, a_coarse, g_level, g_base)])
+        )(*[pltpu.with_memory_space_constraint(x, pltpu.HBM) for x in (image, a_fine, a_rim, a_coarse, g_level, g_base)])
         coarse_ring = strip + 8
         return pl.pallas_call(
             functools.partial(finish, rows_total),
@@ -549,10 +581,10 @@
                 jax.ShapeDtypeStruct((4, strip, tile_cols), BF),
                 jax.ShapeDtypeStruct((2, strip, tile_cols), BF),
             ),
-            in_specs=[vmem] * 5,
+            in_specs=[vmem] * 6,
             out_specs=(hbm,) * 4,
             scratch_shapes=[
-                pltpu.VMEM((a_coarse.shape[0], wide), F32),
+                pltpu.VMEM((a_coarse.shape[1], wide), F32),
                 pltpu.VMEM((LEVELS, tiles * coarse_ring, LANE), F32),
                 pltpu.VMEM((2, (tiles + 1) * coarse_ring, LANE), F32),
                 pltpu.VMEM((4, strip, tile_cols), BF),

time: 16.2 us -> 15.1 us (0.932)
  Pallas kernels: 15.4 us -> 14.3 us
    pallas_call x1, Pallas kernels: 13.6 us -> 12.5 us  [local(): pl.pallas_call(functools.partial(kernel, rows_total), out_shape=(pltpu.VM...]
where the time goes in v3:
time: 15.1 us; the launch traced here: 15 us
  Pallas kernels  14.3 us (95%)
  between operations  0.64 us (4%)
    pallas_call x1, Pallas kernels, local(): pl.pallas_call(functools.partial(kernel, rows_total), out_shape=(pltpu.VM...  12.5 us
    pallas_call x1, Pallas kernels, local(): pl.pallas_call(functools.partial(finish, rows_total), out_shape=(jax.Shap...  1.81 us

profile of v3, /device:TPU:1, one launch (start us, length us, event | category | flops | bytes accessed | tf_op | source)
XLA Modules:
  0.0 15.0 jit_solution(8875873840039332731)
XLA Ops:
  0.6 12.5 %shard_map.93 = (bf16[4,64,2048]{2,1,0:T(8,128)(2,1)S(1)}, bf16[2,64,2048]{2,1,0:T(8,128)(2,1)S(1)}, f32[32,2176]{1,0:T(8,128)S(1)}, bf16[16,2176]{1,0:T(8,128)(...) custom-call(f32[64,2048]{1,0:T(8,128)} %image.1, ...), custom_call_target="tpu_custom_call" | custom-call | tf_op jit(solution)/shard_map/pallas_call | solution.py:541
  13.2 1.8 %shard_map.94 = (bf16[4,64,2048]{2,1,0:T(8,128)(2,1)}, bf16[2,64,2048]{2,1,0:T(8,128)(2,1)}, bf16[4,16,2048]{2,1,0:T(8,128)(2,1)}, bf16[2,16,2048]{2,1,0:T(8,128)(2,1)}) custom-call(bf16[4,64,2048]{2,1,0:T(8,128)(2,1)S(1)} %get-tuple-element.10.dog_near, bf16[2,64,2048]{2,1,0:T(8,128)(2,1)S(1)} %get-tuple-element.11.hess_near, ...), custom_call_target="tpu_custom_call" | custom-call | tf_op jit(solution)/shard_map/pallas_call | solution.py:576

commit v4 on v3

--- a/solution.py
+++ b/solution.py
@@ -258,10 +258,11 @@
     whole = pl.ds(0, RIM)
 
     chunks = tiles // CHUNK
-    span = CHUNK * LANE
+    ready_at = [CHUNK * (j + 1) + 1 for j in range(chunks)]
+    arrive_at = [0] + ready_at[:-1] + [tiles]
     to_down, to_up = [], []
     for j in range(chunks):
-        part = pl.ds(j * span, span)
+        part = pl.ds(arrive_at[j] * LANE, (arrive_at[j + 1] - arrive_at[j]) * LANE)
         to_down.append(remote(last.at[whole, part], above.at[whole, part], fsend.at[2 * j], frecv.at[2 * j], r + 1, c))
         to_up.append(
             remote(first.at[whole, part], below.at[whole, part], fsend.at[2 * j + 1], frecv.at[2 * j + 1], r - 1, c)
@@ -274,18 +275,19 @@
     @pl.when(has_down)
     def _():
         to_down_corner.start()
-        to_down[0].start()
 
     @pl.when(has_up)
     def _():
         to_up_corner.start()
-        for send in to_up:
+
+    def start_if(condition, send):
+        @pl.when(condition)
+        def _():
             send.start()
 
-    @pl.when(has_down)
-    def _():
-        for send in to_down[1:]:
-            send.start()
+    for j in range(chunks):
+        start_if(has_down, to_down[j])
+        start_if(has_up, to_up[j])
 
     to_side.start()
 
@@ -334,17 +336,19 @@
             a_fine[...], own_operand(ext, keep, begin, end), preferred_element_type=F32
         )
 
-    def rim_pass(begin, end):
-        vert[0:middle_at, begin * LANE : end * LANE] += jnp.dot(
-            a_rim[...], rim_operand(rim_in_pair, keep, begin, end), preferred_element_type=F32
+    base_rows = 2 * base_edge
+
+    def rim_pass(rows, begin, end):
+        vert[rows, begin * LANE : end * LANE] += jnp.dot(
+            a_rim[rows, :], rim_operand(rim_in_pair, keep, begin, end), preferred_element_type=F32
         )
 
     rim_in_pair = [above, below]
-    ready_at = [CHUNK * (j + 1) + (1 if j == chunks - 1 else 0) for j in range(chunks)]
+    start_at = [0] + ready_at[:-1]
     base_at = [0] + [(ready - 1) // 2 for ready in ready_at]
     block_at = [0] + [ready - 1 for ready in ready_at[:-1]] + [tiles + 1]
     for j in range(chunks):
-        own_pass(CHUNK * j, ready_at[j])
+        own_pass(start_at[j], ready_at[j])
         base_pass(
             middle_at, half_rows - 2 * base_edge, [(base_edge, half_rows - 2 * base_edge)], base_at[j], base_at[j + 1]
         )
@@ -372,9 +376,9 @@
         def _():
             to_up[j].wait_recv()
 
-        rim_pass(CHUNK * j, ready_at[j])
+        rim_pass(slice(0, base_rows), start_at[j], ready_at[j])
         base_pass(
-            0, 2 * base_edge, [(0, base_edge), (half_rows - base_edge, base_edge)], base_at[j], base_at[j + 1]
+            0, base_rows, [(0, base_edge), (half_rows - base_edge, base_edge)], base_at[j], base_at[j + 1]
         )
 
         columns = (base_at[j + 1] - base_at[j]) * LANE
@@ -403,8 +407,13 @@
 
         pair.start()
         cext[:, mine] = base[:, near]
+
+    for j in range(chunks):
+        rim_pass(slice(base_rows, middle_at), start_at[j], ready_at[j])
+
+    for j in range(chunks):
         horizontal_pass(
-            vert, g_level, lev, 2 * base_edge, edge_rows, edge_pieces, high_rows, block_at[j], block_at[j + 1]
+            vert, g_level, lev, base_rows, edge_rows, edge_pieces, high_rows, block_at[j], block_at[j + 1]
         )
 
     edge_keep = jnp.where(lane == jnp.where(c == 0, 0, LANE - 1), 1.0, 0.0).astype(F32)

time: 15.1 us -> 14 us (0.927)
  Pallas kernels: 14.3 us -> 13.2 us
    pallas_call x1, Pallas kernels: 12.5 us -> 11.4 us  [local(): pl.pallas_call(functools.partial(kernel, rows_total), out_shape=(pltpu.VM...]
where the time goes in v4:
time: 14 us; the launch traced here: 13.8 us
  Pallas kernels  13.2 us (94%)
  between operations  0.64 us (5%)
    pallas_call x1, Pallas kernels, local(): pl.pallas_call(functools.partial(kernel, rows_total), out_shape=(pltpu.VM...  11.4 us
    pallas_call x1, Pallas kernels, local(): pl.pallas_call(functools.partial(finish, rows_total), out_shape=(jax.Shap...  1.81 us

profile of v4, /device:TPU:1, one launch (start us, length us, event | category | flops | bytes accessed | tf_op | source)
XLA Modules:
  0.0 13.8 jit_solution(2435354430050920039)
XLA Ops:
  0.6 11.4 %shard_map.93 = (bf16[4,64,2048]{2,1,0:T(8,128)(2,1)S(1)}, bf16[2,64,2048]{2,1,0:T(8,128)(2,1)S(1)}, f32[32,2176]{1,0:T(8,128)S(1)}, bf16[16,2176]{1,0:T(8,128)(...) custom-call(f32[64,2048]{1,0:T(8,128)} %image.1, ...), custom_call_target="tpu_custom_call" | custom-call | tf_op jit(solution)/shard_map/pallas_call | solution.py:550
  12.0 1.8 %shard_map.94 = (bf16[4,64,2048]{2,1,0:T(8,128)(2,1)}, bf16[2,64,2048]{2,1,0:T(8,128)(2,1)}, bf16[4,16,2048]{2,1,0:T(8,128)(2,1)}, bf16[2,16,2048]{2,1,0:T(8,128)(2,1)}) custom-call(bf16[4,64,2048]{2,1,0:T(8,128)(2,1)S(1)} %get-tuple-element.10.dog_near, bf16[2,64,2048]{2,1,0:T(8,128)(2,1)S(1)} %get-tuple-element.11.hess_near, ...), custom_call_target="tpu_custom_call" | custom-call | tf_op jit(solution)/shard_map/pallas_call | solution.py:585

commit v5 on v4

--- a/solution.py
+++ b/solution.py
@@ -17,7 +17,7 @@
 SPARE = RIM - NEED
 EDGE = 16
 RING = 8
-CHUNK = 4
+CHUNK = 8
 MESH = pl.DeviceIdType.MESH
 BF = jnp.bfloat16
 F32 = jnp.float32

time: 14 us -> 13.5 us (0.964)
  Pallas kernels: 13.2 us -> 12.7 us
    pallas_call x1, Pallas kernels: 11.4 us -> 10.9 us  [local(): pl.pallas_call(functools.partial(kernel, rows_total), out_shape=(pltpu.VM...]
where the time goes in v5:
time: 13.5 us; the launch traced here: 13.4 us
  Pallas kernels  12.7 us (94%)
  between operations  0.64 us (5%)
    pallas_call x1, Pallas kernels, local(): pl.pallas_call(functools.partial(kernel, rows_total), out_shape=(pltpu.VM...  10.9 us
    pallas_call x1, Pallas kernels, local(): pl.pallas_call(functools.partial(finish, rows_total), out_shape=(jax.Shap...  1.81 us

profile of v5, /device:TPU:1, one launch (start us, length us, event | category | flops | bytes accessed | tf_op | source)
XLA Modules:
  0.0 13.4 jit_solution(4266038103354832956)
XLA Ops:
  0.6 10.9 %shard_map.93 = (bf16[4,64,2048]{2,1,0:T(8,128)(2,1)S(1)}, bf16[2,64,2048]{2,1,0:T(8,128)(2,1)S(1)}, f32[32,2176]{1,0:T(8,128)S(1)}, bf16[16,2176]{1,0:T(8,128)(...) custom-call(f32[64,2048]{1,0:T(8,128)} %image.1, ...), custom_call_target="tpu_custom_call" | custom-call | tf_op jit(solution)/shard_map/pallas_call | solution.py:550
  11.5 1.8 %shard_map.94 = (bf16[4,64,2048]{2,1,0:T(8,128)(2,1)}, bf16[2,64,2048]{2,1,0:T(8,128)(2,1)}, bf16[4,16,2048]{2,1,0:T(8,128)(2,1)}, bf16[2,16,2048]{2,1,0:T(8,128)(2,1)}) custom-call(bf16[4,64,2048]{2,1,0:T(8,128)(2,1)S(1)} %get-tuple-element.10.dog_near, bf16[2,64,2048]{2,1,0:T(8,128)(2,1)S(1)} %get-tuple-element.11.hess_near, ...), custom_call_target="tpu_custom_call" | custom-call | tf_op jit(solution)/shard_map/pallas_call | solution.py:585
